TPU v7x, 32 devices: a whole 2x2x4 slice. The times are simulated.
32 devices in a mesh: wide: 16 (over z, x, core), narrow: 2 (over y).
Axes of the slice: x: 2, y: 2, z: 4, core: 2. Of those that a mesh axis runs over, the one named last changes fastest.
Arguments:
- coords: float32 [3, 16, 2048], P(None, 'narrow', 'wide'), may hold values from -1 to 1
- member: int32 [16, 2048], P('narrow', 'wide'), may hold values 0 or 1
- start_vector: float32 [3, 16, 2048], P(None, 'narrow', 'wide'), may hold values from -6 to 6
- self_block: float32 [3, 3, 16, 2048], P(None, None, 'narrow', 'wide'), may hold values from -3 to 141
- neighbour_block: float32 [6, 3, 3, 16, 2048], P(None, None, None, 'narrow', 'wide'), may hold values from -3 to 3
- neighbours: int32 [6, 16, 2048], P(None, 'narrow', 'wide'), may hold values from 0 to 7, as said below
- coarse_map: int32 [512], replicated, may hold values from 0 to 511, each once
Outputs:
- smoothed: float32 [7, 6, 3, 16, 2048], P(None, None, None, 'narrow', 'wide')
- probe_vector: float32 [3, 16, 2048], P(None, 'narrow', 'wide')
- coarse_basis: float32 [36, 512], P(None, ('wide', 'narrow'))
Inputs may be any that keep to these rules, and one draw needn't show every extreme that they name: `neighbours`: the 6 codes of each node are different. `coarse_map`: each aggregate number appears once.
All inputs are finite; a program needn't handle non-finite values. No bound on the sum of `member` on one device may be relied on, other than what follows from the above.
Results may differ from a plain program's by a relative error of at most 0.0003.
Values sent between devices are 32-bit elements; how exact they have to be, the bound alone decides.
A program may use at most 64 MiB of HBM per device.

v0:
```python
import jax
import jax.numpy as jnp
from jax import lax
from jax.sharding import PartitionSpec as P

TILE = 8
ITERS = 4


def extended_2(array, sides, width):
    for axis, dim in sides:
        devices, length = (lax.axis_size(axis), array.shape[dim])
        up = [(i, (i + 1) % devices) for i in range(devices - 1)]
        down = [(j, i) for i, j in up]
        last = lax.slice_in_dim(array, length - width, length, axis=dim)
        initial = lax.slice_in_dim(array, 0, width, axis=dim)
        before = lax.ppermute(last, axis, up)
        after = lax.ppermute(initial, axis, down)
        array = jnp.concatenate([before, array, after], axis=dim)
    return array


def edge_pieces(extended, self_block, neighbour_block, neighbours):
    row_count, col_count = (self_block.shape[2], self_block.shape[3])
    centre = extended[:, :, 1:-1, 1:-1]
    displaced = []
    for code in range(8):
        lifted = code + (1 if code >= 4 else 0)
        step_y = lifted // 3 - 1
        step_x = lifted % 3 - 1
        displaced.append(
            extended[:, :, 1 + step_y : 1 + step_y + row_count, 1 + step_x : 1 + step_x + col_count]
        )
    pieces = [jnp.sum(self_block[None] * centre[:, None], axis=2)]
    for edge_id in range(neighbours.shape[0]):
        picked = displaced[0]
        for code in range(1, 8):
            picked = jnp.where(neighbours[edge_id] == code, displaced[code], picked)
        pieces.append(jnp.sum(neighbour_block[edge_id][None] * picked[:, None], axis=2))
    return pieces


def summed(pieces):
    result = pieces[0]
    for addend in pieces[1:]:
        result = result + addend
    return result


def build_tentative(coords, member):
    present = member.astype(jnp.float32)
    coord_x = coords[0] * present
    coord_y = coords[1] * present
    coord_z = coords[2] * present
    blanks = jnp.zeros_like(present)
    mode_basis = jnp.stack(
        [
            jnp.stack([present, blanks, blanks]),
            jnp.stack([blanks, present, blanks]),
            jnp.stack([blanks, blanks, present]),
            jnp.stack([-coord_y, coord_x, blanks]),
            jnp.stack([blanks, -coord_z, coord_y]),
            jnp.stack([coord_z, blanks, -coord_x]),
        ]
    )
    row_count, col_count = present.shape
    tiles_y, tiles_x = (row_count // TILE, col_count // TILE)
    tiled = mode_basis.reshape(6, 3, tiles_y, TILE, tiles_x, TILE)
    blocks = jnp.transpose(tiled, (2, 4, 0, 1, 3, 5)).reshape(tiles_y, tiles_x, 6, 3 * TILE * TILE)
    gram_matrix = jnp.einsum("yxmr,yxnr->yxmn", blocks, blocks, precision=lax.Precision.HIGHEST)
    factor_low = jnp.linalg.cholesky(gram_matrix)
    orthonormal = jax.scipy.linalg.solve_triangular(factor_low, blocks, lower=True)
    reshaped = orthonormal.reshape(tiles_y, tiles_x, 6, 3, TILE, TILE)
    tentative = jnp.transpose(reshaped, (2, 3, 0, 4, 1, 5)).reshape(6, 3, row_count, col_count)
    return (tentative, factor_low)


def power_image(iterate, self_block, neighbour_block, neighbours):
    extended = extended_2(iterate, (("wide", 3), ("narrow", 2)), 1)
    return summed(edge_pieces(extended, self_block, neighbour_block, neighbours))


def local(coords, member, start_vector, self_block, neighbour_block, neighbours, coarse_map):
    diagonal = jnp.stack([self_block[0, 0], self_block[1, 1], self_block[2, 2]])
    tentative, factor_low = build_tentative(coords, member)
    tentative_ext = extended_2(tentative, (("wide", 3), ("narrow", 2)), 1)
    iterate = start_vector[None]
    curvatures = []
    energies = []
    for number in range(ITERS):
        applied = power_image(iterate, self_block, neighbour_block, neighbours)
        curvatures.append(jnp.sum(iterate * applied))
        energies.append(jnp.sum(iterate * diagonal * iterate))
        iterate = applied / diagonal
    curvature_all, energy_all = lax.psum(
        (jnp.stack(curvatures), jnp.stack(energies)), ("wide", "narrow")
    )
    growth = jnp.float32(1.0)
    for number in range(ITERS):
        growth = growth * (energy_all[number] / curvature_all[number])
    iterate = growth * iterate
    jacobi_weight = 4.0 * energy_all[ITERS - 1] / (3.0 * curvature_all[ITERS - 1])
    pieces = edge_pieces(tentative_ext, self_block, neighbour_block, neighbours)
    weighting = jacobi_weight / diagonal
    smoothed = jnp.stack(
        [tentative - weighting * pieces[0]] + [-weighting * portion for portion in pieces[1:]]
    )
    tiles_y, tiles_x = (factor_low.shape[0], factor_low.shape[1])
    factor_up = jnp.transpose(
        jnp.swapaxes(factor_low, 2, 3).reshape(tiles_y, tiles_x, 36), (2, 0, 1)
    )
    wide_count = lax.axis_size("wide")
    narrow_count = lax.axis_size("narrow")
    share = coarse_map.shape[0] // (wide_count * narrow_count)
    across = tiles_x * wide_count
    gathered = lax.all_gather(
        factor_up.reshape(36, tiles_y * tiles_x), ("wide", "narrow"), axis=1, tiled=True
    )
    owner = lax.axis_index("wide") * narrow_count + lax.axis_index("narrow")
    wanted = lax.dynamic_slice_in_dim(coarse_map, owner * share, share, 0)
    tile_row = wanted // across
    tile_col = wanted % across
    device_id = tile_col // tiles_x * narrow_count + tile_row // tiles_y
    position = (device_id * tiles_y + tile_row % tiles_y) * tiles_x + tile_col % tiles_x
    coarse_basis = jnp.take(gathered, position, axis=1)
    return (smoothed, iterate[0], coarse_basis)


def solution(mesh):
    return jax.shard_map(
        local,
        mesh=mesh,
        in_specs=(
            P(None, "narrow", "wide"),
            P("narrow", "wide"),
            P(None, "narrow", "wide"),
            P(None, None, "narrow", "wide"),
            P(None, None, None, "narrow", "wide"),
            P(None, "narrow", "wide"),
            P(),
        ),
        out_specs=(
            P(None, None, None, "narrow", "wide"),
            P(None, "narrow", "wide"),
            P(None, ("wide", "narrow")),
        ),
        check_vma=False,
    )
```

profile of v0, /device:TPU:0, one launch (start us, length us, event | category | flops | bytes accessed | tf_op | source)
XLA Modules:
  0.0 211.0 jit_solution(10149535950463436135)
XLA Ops:
  0.6 0.9 fusion.34
  1.5 1.3 collective-permute-start.1
  2.8 3.0 %collective-permute-start = (f32[1,3,8,1]{3,2,1,0:T(8,128)S(1)}, f32[1,3,8,1]{3,2,1,0:T(8,128)S(1)}, u32[]{:S(2)}, u32[]{:S(2)}) collective-permute-start(f32[1,3,8,1]{3,2,1,0:T(8,128)S(1)} %get-tuple-element.179), channel_id=1, source_target_pairs={{0,2},{2,4},{4,6},{6,8},{8,10},{10,12},{12,14},{14,16},{16,18},{18... | collective-permute-start | bytes 296 | tf_op jit(solution)/shard_map/ppermute | solution.py:17
  5.8 0.7 fusion.36
  6.5 0.1 stack.105
  6.8 0.1 stack.110
  6.9 0.7 fusion.27
  8.3 0.3 copy.88
  8.7 0.3 copy.89
  9.0 0.2 fusion.39
  9.3 0.2 copy.92
  9.5 8.8 %custom-call.8 = f32[1,16,6,6]{3,2,1,0:T(8,128)S(1)} custom-call(f32[1,16,6,6]{3,2,1,0:T(8,128)S(1)} %fusion.12), custom_call_target="Cholesky" | custom-call | tf_op jit(solution)/shard_map/jit(cholesky)/cholesky | solution.py:71
  18.5 0.1 fusion.15
  18.6 7.6 %custom-call.9 = f32[16,1,6,6]{2,3,1,0:T(8,128)S(1)} custom-call(f32[16,1,6,6]{3,2,1,0:T(8,128)S(1)} %get-tuple-element.111), custom_call_target="InvertDiagBlocksLowerTriangular" | custom-call | tf_op jit(solution)/shard_map/jit(_solve_triangular)/vmap()/triangular_solve | solution.py:72
  26.2 0.4 fusion.13
  26.5 0.2 copy.97
  26.8 0.4 copy.98
  27.2 0.6 mul.701
  27.9 1.3 collective-permute-start.17
  29.2 5.1 %collective-permute-start.16 = (f32[6,3,8,1]{3,2,1,0:T(8,128)S(1)}, f32[6,3,8,1]{3,2,1,0:T(8,128)S(1)}, u32[]{:S(2)}, u32[]{:S(2)}) collective-permute-start(f32[6,3,8,1]{3,2,1,0:T(8,128)S(1)} %get-tuple-element.108), channel_id=1, source_target_pairs={{0,2},{2,4},{4,6},{6,8},{8,10},{10,12},{12,14},{14,16},{16,18},{18... | collective-permute-start | bytes 1736 | tf_op jit(solution)/shard_map/ppermute | solution.py:17
  34.4 0.1 copy.100
  34.6 68.5 %all-gather = f32[36,1,512]{0,2,1:T(8,128)S(1)} all-gather(f32[36,1,16]{0,2,1:T(8,128)S(1)} %bitcast.265), channel_id=2, replica_groups=mesh['wide'=16,'narrow'=2] {'wide','narrow'}, dimensions={2}, use_global_device_ids=true | all-gather | bytes 76032 | tf_op jit(solution)/shard_map/all_gather | solution.py:116
  103.2 0.8 compare_and_fusion
  104.0 0.6 gather_fusion
  104.5 0.7 select_bitcast_fusion.25
  105.2 0.6 reshape.1131
  105.8 0.1 pad_maximum_fusion.80
  105.9 1.3 collective-permute-start.3
  107.2 1.3 collective-permute-start.2
  108.5 0.2 pad_maximum_fusion.18
  108.7 4.5 %collective-permute-start.19 = (f32[6,3,1,130]{3,2,1,0:T(1,128)S(1)}, f32[6,3,1,130]{3,2,1,0:T(1,128)S(1)}, u32[]{:S(2)}, u32[]{:S(2)}) collective-permute-start(f32[6,3,1,130]{3,2,1,0:T(1,128)S(1)} %get-tuple-element.107), channel_id=1, source_target_pairs={{0,1},{2,3},{4,5},{6,7},{8,9},{10,11},{12,13},{14,15},{16,17},{18,... | collective-permute-start | bytes 28088 | tf_op jit(solution)/shard_map/ppermute | solution.py:17
  113.2 0.1 select_bitcast_fusion.20
  113.6 1.3 collective-permute-start.5
  114.9 3.0 %collective-permute-start.4 = (f32[1,3,8,1]{3,2,1,0:T(8,128)S(1)}, f32[1,3,8,1]{3,2,1,0:T(8,128)S(1)}, u32[]{:S(2)}, u32[]{:S(2)}) collective-permute-start(f32[1,3,8,1]{3,2,1,0:T(8,128)S(1)} %get-tuple-element.177), channel_id=1, source_target_pairs={{0,2},{2,4},{4,6},{6,8},{8,10},{10,12},{12,14},{14,16},{16,18},{18... | collective-permute-start | bytes 296 | tf_op jit(solution)/shard_map/ppermute | solution.py:17
  118.0 0.8 collective-permute-done.4
  118.8 0.1 pad_maximum_fusion.77
  118.9 1.3 collective-permute-start.7
  120.2 1.3 collective-permute-start.6
  121.5 4.2 %collective-permute-done.6 = f32[1,3,1,130]{3,2,1,0:T(1,128)S(1)} collective-permute-done((f32[1,3,1,130]{3,2,1,0:T(1,128)S(1)}, f32[1,3,1,130]{3,2,1,0:T(1,128)S(1)}, u32[]{:S(2)}, u32[]{:S(2)}) %collective-permute-start.6) | collective-permute-done | bytes 1592 | tf_op jit(solution)/shard_map/ppermute | solution.py:18
  125.7 0.1 select_bitcast_fusion.13
  126.0 1.3 collective-permute-start.9
  127.3 3.0 %collective-permute-start.8 = (f32[1,3,8,1]{3,2,1,0:T(8,128)S(1)}, f32[1,3,8,1]{3,2,1,0:T(8,128)S(1)}, u32[]{:S(2)}, u32[]{:S(2)}) collective-permute-start(f32[1,3,8,1]{3,2,1,0:T(8,128)S(1)} %get-tuple-element.175), channel_id=1, source_target_pairs={{0,2},{2,4},{4,6},{6,8},{8,10},{10,12},{12,14},{14,16},{16,18},{18... | collective-permute-start | bytes 296 | tf_op jit(solution)/shard_map/ppermute | solution.py:17
  130.4 0.8 collective-permute-done.8
  131.3 1.7 collective-permute-start.11
  132.9 1.3 collective-permute-start.10
  134.2 4.2 %collective-permute-done.10 = f32[1,3,1,130]{3,2,1,0:T(1,128)S(1)} collective-permute-done((f32[1,3,1,130]{3,2,1,0:T(1,128)S(1)}, f32[1,3,1,130]{3,2,1,0:T(1,128)S(1)}, u32[]{:S(2)}, u32[]{:S(2)}) %collective-permute-start.10) | collective-permute-done | bytes 1592 | tf_op jit(solution)/shard_map/ppermute | solution.py:18
  138.4 0.1 select_bitcast_fusion.7
  138.7 0.7 multiply_reduce_fusion.38
  139.5 1.3 collective-permute-start.13
  140.8 3.0 %collective-permute-start.12 = (f32[1,3,8,1]{3,2,1,0:T(8,128)S(1)}, f32[1,3,8,1]{3,2,1,0:T(8,128)S(1)}, u32[]{:S(2)}, u32[]{:S(2)}) collective-permute-start(f32[1,3,8,1]{3,2,1,0:T(8,128)S(1)} %get-tuple-element.173), channel_id=1, source_target_pairs={{0,2},{2,4},{4,6},{6,8},{8,10},{10,12},{12,14},{14,16},{16,18},{18... | collective-permute-start | bytes 296 | tf_op jit(solution)/shard_map/ppermute | solution.py:17
  143.8 0.8 collective-permute-done.12
  144.7 1.8 collective-permute-start.15
  146.5 1.3 collective-permute-start.14
  147.8 2.7 %pad_maximum_fusion.81 = f32[4]{0:T(128)S(1)} fusion(f32[1]{0:T(128)} %bitcast.88, f32[1]{0:T(128)} %bitcast.80, f32[1]{0:T(128)} %bitcast.72, f32[1]{0:T(128)} %bitcast.22), kind=kLoop, calls=%fused_computation.267 | loop fusion | flops 12 | bytes 32 | tf_op jit(solution)/shard_map/stack | solution.py:96
  150.5 1.5 collective-permute-done.14
  152.0 0.1 select_bitcast_fusion.1
  152.3 0.6 multiply_reduce_fusion.35
  152.9 2.6 %pad_maximum_fusion.82 = f32[4]{0:T(128)S(1)} fusion(f32[1]{0:T(128)} %bitcast.99, f32[1]{0:T(128)} %bitcast.91, f32[1]{0:T(128)} %bitcast.90, f32[1]{0:T(128)} %bitcast.89), kind=kLoop, calls=%fused_computation.268 | loop fusion | flops 12 | bytes 32 | tf_op jit(solution)/shard_map/stack | solution.py:96
  155.5 1.3 collective-permute-start.18
  156.8 44.7 %all-reduce.2 = (f32[4]{0:T(128)S(1)}, f32[4]{0:T(128)S(1)}) all-reduce(f32[4]{0:T(128)S(1)} %pad_maximum_fusion.81, f32[4]{0:T(128)S(1)} %pad_maximum_fusion.82), channel_id=1, replica_groups=mesh['wide'=16,'narrow'=2] {'wide','narrow'}, use_global_device_ids=true, to_apply=%region_27.28 | all-reduce | flops 8 | bytes 64 | tf_op jit(solution)/shard_map/psum | solution.py:95
  201.5 0.7 fusion.37
  208.6 0.6 fusion.24
  209.3 0.4 select_select_fusion
  210.2 0.8 copy-done.4
  (106 shorter events, 2.6 us)
Async XLA Ops:
  1.5 104.3 %collective-permute-start.1 = (f32[1,3,8,1]{3,2,1,0:T(8,128)S(1)}, f32[1,3,8,1]{3,2,1,0:T(8,128)S(1)}, u32[]{:S(2)}, u32[]{:S(2)}) collective-permute-start(f32[1,3,8,1]{3,2,1,0:T(8,128)S(1)} %get-tuple-element.180), channel_id=1, source_target_pairs={{2,0},{4,2},{6,4},{8,6},{10,8},{12,10},{14,12},{16,14},{18,16},{20... | collective-permute-start | bytes 296 | tf_op jit(solution)/shard_map/ppermute | solution.py:18
  2.8 103.0 %collective-permute-start = (f32[1,3,8,1]{3,2,1,0:T(8,128)S(1)}, f32[1,3,8,1]{3,2,1,0:T(8,128)S(1)}, u32[]{:S(2)}, u32[]{:S(2)}) collective-permute-start(f32[1,3,8,1]{3,2,1,0:T(8,128)S(1)} %get-tuple-element.179), channel_id=1, source_target_pairs={{0,2},{2,4},{4,6},{6,8},{8,10},{10,12},{12,14},{14,16},{16,18},{18... | collective-permute-start | bytes 296 | tf_op jit(solution)/shard_map/ppermute | solution.py:17
  27.2 7.1 %copy-start.1 = (f32[3,3,8,128]{3,2,1,0:T(8,128)S(1)}, f32[3,3,8,128]{3,2,1,0:T(8,128)}, u32[]{:S(2)}) copy-start(f32[3,3,8,128]{3,2,1,0:T(8,128)} %param.10) | copy-start | bytes 110596
  27.2 7.1 %copy-start.3 = (s32[6,8,128]{2,1,0:T(8,128)S(1)}, s32[6,8,128]{2,1,0:T(8,128)}, u32[]{:S(2)}) copy-start(s32[6,8,128]{2,1,0:T(8,128)} %param.12) | copy-start | bytes 73732
  27.2 7.2 %copy-start.2 = (f32[3,8,128]{2,1,0:T(8,128)S(1)}, f32[3,8,128]{2,1,0:T(8,128)}, u32[]{:S(2)}) copy-start(f32[3,8,128]{2,1,0:T(8,128)} %param.9) | copy-start | bytes 36868
  27.9 80.6 %collective-permute-start.17 = (f32[6,3,8,1]{3,2,1,0:T(8,128)S(1)}, f32[6,3,8,1]{3,2,1,0:T(8,128)S(1)}, u32[]{:S(2)}, u32[]{:S(2)}) collective-permute-start(f32[6,3,8,1]{3,2,1,0:T(8,128)S(1)} %get-tuple-element.109), channel_id=1, source_target_pairs={{2,0},{4,2},{6,4},{8,6},{10,8},{12,10},{14,12},{16,14},{18,16},{20... | collective-permute-start | bytes 1736 | tf_op jit(solution)/shard_map/ppermute | solution.py:18
  29.2 79.3 %collective-permute-start.16 = (f32[6,3,8,1]{3,2,1,0:T(8,128)S(1)}, f32[6,3,8,1]{3,2,1,0:T(8,128)S(1)}, u32[]{:S(2)}, u32[]{:S(2)}) collective-permute-start(f32[6,3,8,1]{3,2,1,0:T(8,128)S(1)} %get-tuple-element.108), channel_id=1, source_target_pairs={{0,2},{2,4},{4,6},{6,8},{8,10},{10,12},{12,14},{14,16},{16,18},{18... | collective-permute-start | bytes 1736 | tf_op jit(solution)/shard_map/ppermute | solution.py:17
  105.2 8.3 %copy-start = (f32[6,3,3,8,128]{4,3,2,1,0:T(8,128)S(1)}, f32[6,3,3,8,128]{4,3,2,1,0:T(8,128)}, u32[]{:S(2)}) copy-start(f32[6,3,3,8,128]{4,3,2,1,0:T(8,128)} %param.11) | copy-start | bytes 663556
  105.9 7.4 %collective-permute-start.3 = (f32[1,3,1,130]{3,2,1,0:T(1,128)S(1)}, f32[1,3,1,130]{3,2,1,0:T(1,128)S(1)}, u32[]{:S(2)}, u32[]{:S(2)}) collective-permute-start(f32[1,3,1,130]{3,2,1,0:T(1,128)S(1)} %get-tuple-element.119), channel_id=1, source_target_pairs={{0,1},{2,3},{4,5},{6,7},{8,9},{10,11},{12,13},{14,15},{16,17},{18,... | collective-permute-start | bytes 4688 | tf_op jit(solution)/shard_map/ppermute | solution.py:17
  107.2 6.1 %collective-permute-start.2 = (f32[1,3,1,130]{3,2,1,0:T(1,128)S(1)}, f32[1,3,1,130]{3,2,1,0:T(1,128)S(1)}, u32[]{:S(2)}, u32[]{:S(2)}) collective-permute-start(f32[1,3,1,130]{3,2,1,0:T(1,128)S(1)} %get-tuple-element.118), channel_id=1, source_target_pairs={{1,0},{3,2},{5,4},{7,6},{9,8},{11,10},{13,12},{15,14},{17,16},{19,... | collective-permute-start | bytes 4688 | tf_op jit(solution)/shard_map/ppermute | solution.py:18
  108.7 100.6 %collective-permute-start.19 = (f32[6,3,1,130]{3,2,1,0:T(1,128)S(1)}, f32[6,3,1,130]{3,2,1,0:T(1,128)S(1)}, u32[]{:S(2)}, u32[]{:S(2)}) collective-permute-start(f32[6,3,1,130]{3,2,1,0:T(1,128)S(1)} %get-tuple-element.107), channel_id=1, source_target_pairs={{0,1},{2,3},{4,5},{6,7},{8,9},{10,11},{12,13},{14,15},{16,17},{18,... | collective-permute-start | bytes 28088 | tf_op jit(solution)/shard_map/ppermute | solution.py:17
  113.6 4.3 %collective-permute-start.5 = (f32[1,3,8,1]{3,2,1,0:T(8,128)S(1)}, f32[1,3,8,1]{3,2,1,0:T(8,128)S(1)}, u32[]{:S(2)}, u32[]{:S(2)}) collective-permute-start(f32[1,3,8,1]{3,2,1,0:T(8,128)S(1)} %get-tuple-element.178), channel_id=1, source_target_pairs={{2,0},{4,2},{6,4},{8,6},{10,8},{12,10},{14,12},{16,14},{18,16},{20... | collective-permute-start | bytes 296 | tf_op jit(solution)/shard_map/ppermute | solution.py:18
  114.9 3.9 %collective-permute-start.4 = (f32[1,3,8,1]{3,2,1,0:T(8,128)S(1)}, f32[1,3,8,1]{3,2,1,0:T(8,128)S(1)}, u32[]{:S(2)}, u32[]{:S(2)}) collective-permute-start(f32[1,3,8,1]{3,2,1,0:T(8,128)S(1)} %get-tuple-element.177), channel_id=1, source_target_pairs={{0,2},{2,4},{4,6},{6,8},{8,10},{10,12},{12,14},{14,16},{16,18},{18... | collective-permute-start | bytes 296 | tf_op jit(solution)/shard_map/ppermute | solution.py:17
  118.9 2.6 %collective-permute-start.7 = (f32[1,3,1,130]{3,2,1,0:T(1,128)S(1)}, f32[1,3,1,130]{3,2,1,0:T(1,128)S(1)}, u32[]{:S(2)}, u32[]{:S(2)}) collective-permute-start(f32[1,3,1,130]{3,2,1,0:T(1,128)S(1)} %get-tuple-element.117), channel_id=1, source_target_pairs={{0,1},{2,3},{4,5},{6,7},{8,9},{10,11},{12,13},{14,15},{16,17},{18,... | collective-permute-start | bytes 4688 | tf_op jit(solution)/shard_map/ppermute | solution.py:17
  120.2 5.5 %collective-permute-start.6 = (f32[1,3,1,130]{3,2,1,0:T(1,128)S(1)}, f32[1,3,1,130]{3,2,1,0:T(1,128)S(1)}, u32[]{:S(2)}, u32[]{:S(2)}) collective-permute-start(f32[1,3,1,130]{3,2,1,0:T(1,128)S(1)} %get-tuple-element.116), channel_id=1, source_target_pairs={{1,0},{3,2},{5,4},{7,6},{9,8},{11,10},{13,12},{15,14},{17,16},{19,... | collective-permute-start | bytes 4688 | tf_op jit(solution)/shard_map/ppermute | solution.py:18
  126.0 4.3 %collective-permute-start.9 = (f32[1,3,8,1]{3,2,1,0:T(8,128)S(1)}, f32[1,3,8,1]{3,2,1,0:T(8,128)S(1)}, u32[]{:S(2)}, u32[]{:S(2)}) collective-permute-start(f32[1,3,8,1]{3,2,1,0:T(8,128)S(1)} %get-tuple-element.176), channel_id=1, source_target_pairs={{2,0},{4,2},{6,4},{8,6},{10,8},{12,10},{14,12},{16,14},{18,16},{20... | collective-permute-start | bytes 296 | tf_op jit(solution)/shard_map/ppermute | solution.py:18
  127.3 3.9 %collective-permute-start.8 = (f32[1,3,8,1]{3,2,1,0:T(8,128)S(1)}, f32[1,3,8,1]{3,2,1,0:T(8,128)S(1)}, u32[]{:S(2)}, u32[]{:S(2)}) collective-permute-start(f32[1,3,8,1]{3,2,1,0:T(8,128)S(1)} %get-tuple-element.175), channel_id=1, source_target_pairs={{0,2},{2,4},{4,6},{6,8},{8,10},{10,12},{12,14},{14,16},{16,18},{18... | collective-permute-start | bytes 296 | tf_op jit(solution)/shard_map/ppermute | solution.py:17
  131.3 3.0 %collective-permute-start.11 = (f32[1,3,1,130]{3,2,1,0:T(1,128)S(1)}, f32[1,3,1,130]{3,2,1,0:T(1,128)S(1)}, u32[]{:S(2)}, u32[]{:S(2)}) collective-permute-start(f32[1,3,1,130]{3,2,1,0:T(1,128)S(1)} %get-tuple-element.115), channel_id=1, source_target_pairs={{0,1},{2,3},{4,5},{6,7},{8,9},{10,11},{12,13},{14,15},{16,17},{18,... | collective-permute-start | bytes 4688 | tf_op jit(solution)/shard_map/ppermute | solution.py:17
  132.9 5.5 %collective-permute-start.10 = (f32[1,3,1,130]{3,2,1,0:T(1,128)S(1)}, f32[1,3,1,130]{3,2,1,0:T(1,128)S(1)}, u32[]{:S(2)}, u32[]{:S(2)}) collective-permute-start(f32[1,3,1,130]{3,2,1,0:T(1,128)S(1)} %get-tuple-element.114), channel_id=1, source_target_pairs={{1,0},{3,2},{5,4},{7,6},{9,8},{11,10},{13,12},{15,14},{17,16},{19,... | collective-permute-start | bytes 4688 | tf_op jit(solution)/shard_map/ppermute | solution.py:18
  139.5 4.3 %collective-permute-start.13 = (f32[1,3,8,1]{3,2,1,0:T(8,128)S(1)}, f32[1,3,8,1]{3,2,1,0:T(8,128)S(1)}, u32[]{:S(2)}, u32[]{:S(2)}) collective-permute-start(f32[1,3,8,1]{3,2,1,0:T(8,128)S(1)} %get-tuple-element.174), channel_id=1, source_target_pairs={{2,0},{4,2},{6,4},{8,6},{10,8},{12,10},{14,12},{16,14},{18,16},{20... | collective-permute-start | bytes 296 | tf_op jit(solution)/shard_map/ppermute | solution.py:18
  140.8 3.9 %collective-permute-start.12 = (f32[1,3,8,1]{3,2,1,0:T(8,128)S(1)}, f32[1,3,8,1]{3,2,1,0:T(8,128)S(1)}, u32[]{:S(2)}, u32[]{:S(2)}) collective-permute-start(f32[1,3,8,1]{3,2,1,0:T(8,128)S(1)} %get-tuple-element.173), channel_id=1, source_target_pairs={{0,2},{2,4},{4,6},{6,8},{8,10},{10,12},{12,14},{14,16},{16,18},{18... | collective-permute-start | bytes 296 | tf_op jit(solution)/shard_map/ppermute | solution.py:17
  144.7 5.8 %collective-permute-start.15 = (f32[1,3,1,130]{3,2,1,0:T(1,128)S(1)}, f32[1,3,1,130]{3,2,1,0:T(1,128)S(1)}, u32[]{:S(2)}, u32[]{:S(2)}) collective-permute-start(f32[1,3,1,130]{3,2,1,0:T(1,128)S(1)} %get-tuple-element.113), channel_id=1, source_target_pairs={{0,1},{2,3},{4,5},{6,7},{8,9},{10,11},{12,13},{14,15},{16,17},{18,... | collective-permute-start | bytes 4688 | tf_op jit(solution)/shard_map/ppermute | solution.py:17
  146.5 5.5 %collective-permute-start.14 = (f32[1,3,1,130]{3,2,1,0:T(1,128)S(1)}, f32[1,3,1,130]{3,2,1,0:T(1,128)S(1)}, u32[]{:S(2)}, u32[]{:S(2)}) collective-permute-start(f32[1,3,1,130]{3,2,1,0:T(1,128)S(1)} %get-tuple-element.112), channel_id=1, source_target_pairs={{1,0},{3,2},{5,4},{7,6},{9,8},{11,10},{13,12},{15,14},{17,16},{19,... | collective-permute-start | bytes 4688 | tf_op jit(solution)/shard_map/ppermute | solution.py:18
  155.5 53.8 %collective-permute-start.18 = (f32[6,3,1,130]{3,2,1,0:T(1,128)S(1)}, f32[6,3,1,130]{3,2,1,0:T(1,128)S(1)}, u32[]{:S(2)}, u32[]{:S(2)}) collective-permute-start(f32[6,3,1,130]{3,2,1,0:T(1,128)S(1)} %get-tuple-element.106), channel_id=1, source_target_pairs={{1,0},{3,2},{5,4},{7,6},{9,8},{11,10},{13,12},{15,14},{17,16},{19,... | collective-permute-start | bytes 28088 | tf_op jit(solution)/shard_map/ppermute | solution.py:18
  210.2 0.8 copy-start.4
where the time goes:
time: 212 us; the launch traced here: 211 us
  blocking collectives  113 us (53%)
  starting transfers between devices  40.7 us (19%)
  other arithmetic  29.1 us (14%)
  waiting for transfers between devices  12.3 us (6%)
  between operations  8.01 us (4%)
  local copies, waits for them, and re-layouts  6.97 us (3%)
    all_gather x1, blocking collectives, local(): lax.all_gather(factor_up.reshape(36, tiles_y * tiles_x), ('wide', 'narrow...  68.5 us
    psum x1, blocking collectives, local(): lax.psum((jnp.stack(curvatures), jnp.stack(energies)), ('wide', 'narrow'))  44.7 us
    ppermute x10, starting transfers between devices, extended_2(): before = lax.ppermute(last, axis, up)  27.8 us
    ppermute x10, starting transfers between devices, extended_2(): after = lax.ppermute(initial, axis, down)  12.9 us
    ppermute x10, waiting for transfers between devices, extended_2(): after = lax.ppermute(initial, axis, down)  9.88 us
    another operation x4, other arithmetic, build_tentative(): factor_low = jnp.linalg.cholesky(gram_matrix)  8.89 us
    another operation x2, other arithmetic, build_tentative(): jax.scipy.linalg.solve_triangular(factor_low, blocks, lower=True)  7.57 us
  transfers between devices with their start and end apart: 20, of which 6 were waited for; matrix products, arithmetic and copies ran while one was open for 16% of the time, Pallas kernels for 0%

commit v1 on v0

v1 whole, which is shorter than its diff:
```python
import functools

import jax
import jax.numpy as jnp
from jax import lax
from jax.experimental import pallas as pl
from jax.experimental.pallas import tpu as pltpu
from jax.sharding import PartitionSpec as P

TILE = 8
ITERS = 4
MESH = pl.DeviceIdType.MESH
F32 = jnp.float32
SUMS = 10
FIELDS = 9
STEPS = [(-1, -1), (-1, 0), (-1, 1), (0, -1), (0, 1), (1, -1), (1, 0), (1, 1)]


def roll(x, shift, axis):
    size = x.shape[axis]
    shift = shift % size
    return x if shift == 0 else pltpu.roll(x, shift, axis)


def displaced(v, lcol, rcol, rows, lane, row):
    height, width = v.shape
    first, last = lane == 0, lane == width - 1
    top, bottom = row == 0, row == height - 1
    vl = jnp.where(first, lcol, roll(v, 1, 1))
    vr = jnp.where(last, rcol, roll(v, -1, 1))
    w = jnp.where(bottom, rows[1], rows[6])
    wl = jnp.where(bottom, rows[0], rows[5])
    wr = jnp.where(bottom, rows[2], rows[7])
    wsl = roll(jnp.where(last, wl, w), 1, 1)
    wsr = roll(jnp.where(first, wr, w), -1, 1)
    up = [roll(jnp.where(bottom, b, a), 1, 0) for a, b in ((vl, wsl), (v, w), (vr, wsr))]
    down = [roll(jnp.where(top, b, a), -1, 0) for a, b in ((vl, wsl), (v, w), (vr, wsr))]
    return up + [vl, vr] + down


def kernel(
    wide, narrow, share,
    coords_h, member_h, start_h, self_h, nb_h, nbr_h, cmap_h,
    out_ref, probe_ref, coarse_ref,
    coords, member, selfb, nb, nbr, cmap,
    its, edges, stencil, fields, pack, tedges, disp, mine, gath, sumrow, allsum, partial,
    hrecv, vrecv, htrecv, vtrecv,
    in_sem, send_sem, recv_sem, tsend_sem, trecv_sem, gsend_sem, grecv_sem, ssend_sem, srecv_sem,
):
    count = wide * narrow
    me_w, me_n = lax.axis_index("wide"), lax.axis_index("narrow")
    me = me_w * narrow + me_n
    barrier = pltpu.get_barrier_semaphore()

    def peer(d):
        other = lax.rem(me + d, count)
        return (other // narrow, lax.rem(other, narrow))

    @pl.loop(1, count)
    def _(d):
        pl.semaphore_signal(barrier, inc=1, device_id=peer(d), device_id_type=MESH)

    loads = [
        pltpu.make_async_copy(src, dst, in_sem.at[i])
        for i, (src, dst) in enumerate(
            (
                (coords_h, coords), (member_h, member), (start_h, its.at[0]), (nbr_h, nbr),
                (self_h, selfb), (nb_h, nb), (cmap_h, cmap),
            )
        )
    ]
    for load in loads:
        load.start()

    def exists(code):
        dy, dx = STEPS[code]
        ok = None
        for step, at, size in ((dy, me_n, narrow), (dx, me_w, wide)):
            term = at > 0 if step < 0 else (at < size - 1 if step > 0 else None)
            if term is not None:
                ok = term if ok is None else jnp.logical_and(ok, term)
        return ok

    present_at = [exists(code) for code in range(8)]

    def target(code):
        dy, dx = STEPS[code]
        return (me_w + dx, me_n + dy)

    for code in range(8):
        @pl.when(jnp.logical_not(present_at[code]))
        def _(code=code):
            if code in (3, 4):
                hrecv[:, code - 3] = jnp.zeros(hrecv.shape[:1] + hrecv.shape[2:], F32)
                htrecv[code - 3] = jnp.zeros(htrecv.shape[1:], F32)
            else:
                vrecv[:, code] = jnp.zeros(vrecv.shape[:1] + vrecv.shape[2:], F32)
                vtrecv[code] = jnp.zeros(vtrecv.shape[1:], F32)

    shape = member.shape
    height, width = shape
    lane = lax.broadcasted_iota(jnp.int32, shape, 1)
    row = lax.broadcasted_iota(jnp.int32, shape, 0)

    def edge_rows(values, number):
        for r in range(3):
            edges[number, r : r + 1, :] = values[r][:1]
            edges[number, r + 4 : r + 5, :] = values[r][height - 1 :]

    for load in loads[:4]:
        load.wait()
    start = [its[0, r] for r in range(3)]
    edge_rows(start, 0)
    present = member[...].astype(F32)
    x, y, z = (coords[r] * present for r in range(3))
    products = [present * present, x * present, y * present, z * present, x * x, y * y, z * z, x * y, x * z, y * z]
    tiles = []
    for base in (0, 8):
        tile = jnp.zeros(shape, F32)
        for q, product in enumerate(products[base : base + 8]):
            tile = jnp.where(row == q, jnp.sum(product, axis=0, keepdims=True), tile)
        for s in (1, 2, 4):
            tile = tile + jnp.where((lane & s) != 0, roll(tile, s, 1), roll(tile, -s, 1))
        tiles.append(tile)
    sums = [tiles[q // 8][q % 8 : q % 8 + 1, :] for q in range(SUMS)]

    def factor(sums):
        n, sx, sy, sz, xx, yy, zz, xy, xz, yz = sums
        l00 = jnp.sqrt(n)
        mx, my, mz = sx / l00, sy / l00, sz / l00
        l33 = jnp.sqrt(xx + yy - mx * mx - my * my)
        l43 = (mx * mz - xz) / l33
        l53 = (my * mz - yz) / l33
        l44 = jnp.sqrt(yy + zz - my * my - mz * mz - l43 * l43)
        l54 = (mx * my - xy - l53 * l43) / l44
        l55 = jnp.sqrt(xx + zz - mx * mx - mz * mz - l53 * l53 - l54 * l54)
        return l00, mx, my, mz, l33, l43, l53, l44, l54, l55

    parts = factor(sums)
    l00, mx, my, mz, l33, l43, l53, l44, l54, l55 = parts
    unit = present / l00
    cx, cy, cz = x - mx * unit, y - my * unit, z - mz * unit
    a0, a1 = -cy / l33, cx / l33
    b0, b1, b2 = -l43 * a0 / l44, (-cz - l43 * a1) / l44, cy / l44
    g0 = (cz - l53 * a0 - l54 * b0) / l55
    g1 = (-l53 * a1 - l54 * b1) / l55
    g2 = (-cx - l54 * b2) / l55
    tent = [unit, a0, a1, b0, b1, b2, g0, g1, g2]
    packl, packr = jnp.zeros(shape, F32), jnp.zeros(shape, F32)
    for j, field in enumerate(tent):
        fields[j] = field
        packl = jnp.where(lane == j, roll(field, j, 1), packl)
        packr = jnp.where(lane == j, roll(field, j + 1, 1), packr)
        tedges[0, j : j + 1, :] = field[:1]
        tedges[1, j : j + 1, :] = field[height - 1 :]
    pack[0] = packl
    pack[1] = packr
    lane_row = lax.broadcasted_iota(jnp.int32, (1, width), 1) % 8
    rows_out = []
    for base in (0, 8):
        line = jnp.zeros((1, width), F32)
        for q, part in enumerate(parts[base : base + 8]):
            line = jnp.where(lane_row == q, part, line)
        rows_out.append(line)
    mine[0:1] = rows_out[0]
    mine[1:2] = rows_out[1]
    gath[me] = jnp.concatenate(rows_out, axis=0)

    pl.semaphore_wait(barrier, count - 1)

    def send_halo(number):
        copies = []
        for code in range(8):
            if code in (3, 4):
                src, dst = its.at[number], hrecv.at[number, 4 - code]
            else:
                src, dst = edges.at[number], vrecv.at[number, 7 - code]
            copy = pltpu.make_async_remote_copy(
                src_ref=src, dst_ref=dst, send_sem=send_sem.at[number, code], recv_sem=recv_sem.at[number, 7 - code],
                device_id=target(code), device_id_type=MESH,
            )
            pl.when(present_at[code])(copy.start)
            copies.append(copy)
        return copies

    def wait_halo(number, recv, hbuf, vbuf):
        for code in range(8):
            if code in (3, 4):
                ref = hbuf.at[code - 3]
            else:
                ref = vbuf.at[code]
            arrival = pltpu.make_async_copy(ref, ref, recv(code))
            pl.when(present_at[code])(arrival.wait)

    sent = [send_halo(0)]
    tcopies = []
    for code in range(8):
        if code in (3, 4):
            src, dst = pack.at[code - 3], htrecv.at[4 - code]
        else:
            src, dst = tedges.at[0 if code < 3 else 1], vtrecv.at[7 - code]
        copy = pltpu.make_async_remote_copy(
            src_ref=src, dst_ref=dst, send_sem=tsend_sem.at[code], recv_sem=trecv_sem.at[7 - code],
            device_id=target(code), device_id_type=MESH,
        )
        pl.when(present_at[code])(copy.start)
        tcopies.append(copy)

    @pl.loop(1, count)
    def _(d):
        pltpu.make_async_remote_copy(
            src_ref=mine, dst_ref=gath.at[me], send_sem=gsend_sem, recv_sem=grecv_sem,
            device_id=peer(d), device_id_type=MESH,
        ).start()

    for load in loads[4:]:
        load.wait()
    edge_count = nb.shape[0]
    for code in range(8):
        masks = [nbr[k] == code for k in range(edge_count)]
        for r in range(3):
            for s in range(3):
                value = jnp.zeros(shape, F32)
                for k in range(edge_count):
                    value = jnp.where(masks[k], nb[k, r, s], value)
                stencil[code, 3 * r + s] = value
    diag = [selfb[r, r] for r in range(3)]
    inv = [1.0 / d for d in diag]

    iterate = start
    for number in range(ITERS):
        wait_halo(number, lambda code: recv_sem.at[number, code], hrecv.at[number], vrecv.at[number])
        applied = [sum(selfb[r, s] * iterate[s] for s in range(3)) for r in range(3)]
        for s in range(3):
            rows = {
                code: vrecv[number, code, (s + 4 if code < 3 else s) : (s + 5 if code < 3 else s + 1), :]
                for code in (0, 1, 2, 5, 6, 7)
            }
            moved = displaced(
                iterate[s], roll(hrecv[number, 0, s], 1, 1), roll(hrecv[number, 1, s], -1, 1), rows, lane, row
            )
            for r in range(3):
                for code in range(8):
                    applied[r] = applied[r] + stencil[code, 3 * r + s] * moved[code]
        following = [applied[r] * inv[r] for r in range(3)]
        if number < ITERS - 1:
            for r in range(3):
                its[number + 1, r] = following[r]
            edge_rows(following, number + 1)
            sent.append(send_halo(number + 1))
        curvature = sum(iterate[r] * applied[r] for r in range(3))
        energy = sum(iterate[r] * diag[r] * iterate[r] for r in range(3))
        partial[number : number + 1] = jnp.sum(curvature, axis=0, keepdims=True)
        partial[number + 4 : number + 5] = jnp.sum(energy, axis=0, keepdims=True)
        iterate = following

    totals = jnp.sum(partial[...], axis=1, keepdims=True)
    line = jnp.sum(jnp.where(lane == row, totals, 0.0), axis=0, keepdims=True)
    sumrow[...] = line
    allsum[me] = line

    @pl.loop(1, count)
    def _(d):
        pltpu.make_async_remote_copy(
            src_ref=sumrow, dst_ref=allsum.at[me], send_sem=ssend_sem, recv_sem=srecv_sem,
            device_id=peer(d), device_id_type=MESH,
        ).start()

    wait_halo(0, lambda code: trecv_sem.at[code], htrecv, vtrecv)
    lpack, rpack = htrecv[0], htrecv[1]
    for j in range(FIELDS):
        rows = {code: vtrecv[code, j : j + 1, :] for code in (0, 1, 2, 5, 6, 7)}
        moved = displaced(tent[j], roll(lpack, -j, 1), roll(rpack, width - 1 - j, 1), rows, lane, row)
        for code in range(8):
            disp[j, code] = moved[code]

    def piece(block, picked, index):
        unit, a0, a1, b0, b1, b2, g0, g1, g2 = picked
        for r in range(3):
            c0, c1, c2 = (block(r, s) * -inv[r] for s in range(3))
            out_ref[index, 0, r] = c0 * unit
            out_ref[index, 1, r] = c1 * unit
            out_ref[index, 2, r] = c2 * unit
            out_ref[index, 3, r] = c0 * a0 + c1 * a1
            out_ref[index, 4, r] = c0 * b0 + c1 * b1 + c2 * b2
            out_ref[index, 5, r] = c0 * g0 + c1 * g1 + c2 * g2

    piece(lambda r, s: selfb[r, s], [fields[j] for j in range(FIELDS)], 0)
    for k in range(edge_count):
        masks = [nbr[k] == code for code in range(1, 8)]
        picked = []
        for j in range(FIELDS):
            value = disp[j, 0]
            for code in range(1, 8):
                value = jnp.where(masks[code - 1], disp[j, code], value)
            picked.append(value)
        piece(lambda r, s: nb[k, r, s], picked, k + 1)

    some = gath.at[pl.ds(0, count - 1)]
    pltpu.make_async_copy(some, some, grecv_sem).wait()
    across = width // TILE * wide
    tiles_x, tiles_y = width // TILE, height // TILE
    crow = lax.broadcasted_iota(jnp.int32, (share, width), 0)
    cgroup = lax.broadcasted_iota(jnp.int32, (share, width), 1) // TILE
    low, high = jnp.zeros((share, width), F32), jnp.zeros((share, width), F32)
    for j in range(share):
        wanted = cmap[me * share + j]
        tile_row, tile_col = wanted // across, lax.rem(wanted, across)
        slot = tile_col // tiles_x * narrow + tile_row // tiles_y
        lines = gath[slot]
        take = jnp.logical_and(crow == j, cgroup == lax.rem(tile_col, tiles_x))
        low = jnp.where(take, lines[0:1], low)
        high = jnp.where(take, lines[1:2], high)
    pick = (lax.broadcasted_iota(jnp.int32, (8, width), 1) % 8 == lax.broadcasted_iota(jnp.int32, (8, width), 0)).astype(F32)
    low, high = (
        lax.dot_general(
            pick, v, (((1,), (1,)), ((), ())), precision=lax.Precision.HIGHEST, preferred_element_type=F32
        )
        for v in (low, high)
    )
    l00, mx, my, mz, l33, l43, l53, l44 = (low[q : q + 1] for q in range(8))
    l54, l55 = high[0:1], high[1:2]
    coarse_ref[...] = jnp.zeros(coarse_ref.shape, F32)
    entries = {
        (0, 0): l00, (1, 1): l00, (2, 2): l00,
        (3, 0): -my, (3, 1): mx, (4, 1): -mz, (4, 2): my, (5, 0): mz, (5, 2): -mx,
        (3, 3): l33, (4, 3): l43, (5, 3): l53, (4, 4): l44, (5, 4): l54, (5, 5): l55,
    }
    for (n, m), entry in entries.items():
        coarse_ref[6 * m + n : 6 * m + n + 1, :] = entry

    some = allsum.at[pl.ds(0, count - 1)]
    pltpu.make_async_copy(some, some, srecv_sem).wait()
    if count <= 64:
        lines = [allsum[d] for d in range(count)]
        while len(lines) > 1:
            lines = [a + b for a, b in zip(lines[::2], lines[1::2])] + ([lines[-1]] if len(lines) % 2 else [])
        total = lines[0]
    else:
        total = lax.fori_loop(0, count, lambda d, t: t + allsum[d], jnp.zeros((1, width), F32))
    lane1 = lax.broadcasted_iota(jnp.int32, (1, width), 1)
    ratio = roll(jnp.broadcast_to(total, shape), -4, 1)[:1] / total
    ratios = [jnp.sum(jnp.where(lane1 == i, ratio, 0.0), axis=1, keepdims=True) for i in range(ITERS)]
    growth = ratios[0]
    for i in range(1, ITERS):
        growth = growth * ratios[i]
    weight = jnp.broadcast_to(ratios[ITERS - 1] * (4.0 / 3.0), shape)
    growth = jnp.broadcast_to(growth, shape)
    for r in range(3):
        probe_ref[r] = iterate[r] * growth
    base = {(0, 0): 0, (1, 1): 0, (2, 2): 0, (3, 0): 1, (3, 1): 2}
    for r in range(3):
        base[(4, r)] = 3 + r
        base[(5, r)] = 6 + r
    for m in range(6):
        for r in range(3):
            value = out_ref[0, m, r] * weight
            out_ref[0, m, r] = value + fields[base[(m, r)]] if (m, r) in base else value
    for k in range(1, edge_count + 1):
        for m in range(6):
            for r in range(3):
                out_ref[k, m, r] = out_ref[k, m, r] * weight

    for copies in sent + [tcopies]:
        for code in range(8):
            pl.when(present_at[code])(copies[code].wait_send)
    for buffer, sem in ((gath, gsend_sem), (allsum, ssend_sem)):
        some = buffer.at[pl.ds(0, count - 1)]
        pltpu.make_async_copy(some, some, sem).wait()


def local(wide, narrow, coords, member, start_vector, self_block, neighbour_block, neighbours, coarse_map):
    height, width = member.shape
    edge_count = neighbours.shape[0]
    count = wide * narrow
    share = coarse_map.shape[0] // count
    tile = (height, width)
    vmem = pltpu.VMEM
    dma = pltpu.SemaphoreType.DMA
    return pl.pallas_call(
        functools.partial(kernel, wide, narrow, share),
        out_shape=(
            jax.ShapeDtypeStruct((edge_count + 1, 6, 3) + tile, F32),
            jax.ShapeDtypeStruct((3,) + tile, F32),
            jax.ShapeDtypeStruct((36, share), F32),
        ),
        in_specs=[pl.BlockSpec(memory_space=pl.ANY)] * 7,
        out_specs=(pl.BlockSpec(memory_space=pltpu.VMEM),) * 3,
        scratch_shapes=[
            vmem((3,) + tile, F32),
            vmem(tile, jnp.int32),
            vmem((3, 3) + tile, F32),
            vmem((edge_count, 3, 3) + tile, F32),
            vmem((edge_count,) + tile, jnp.int32),
            pltpu.SMEM(coarse_map.shape, jnp.int32),
            vmem((ITERS, 3) + tile, F32),
            vmem((ITERS, 8, width), F32),
            vmem((8, 9) + tile, F32),
            vmem((FIELDS,) + tile, F32),
            vmem((2,) + tile, F32),
            vmem((2, 16, width), F32),
            vmem((FIELDS, 8) + tile, F32),
            vmem((2, width), F32),
            vmem((count, 2, width), F32),
            vmem((1, width), F32),
            vmem((count, 1, width), F32),
            vmem((8, width), F32),
            vmem((ITERS, 2, 3) + tile, F32),
            vmem((ITERS, 8, 8, width), F32),
            vmem((2,) + tile, F32),
            vmem((8, 16, width), F32),
            dma((7,)),
            dma((ITERS, 8)),
            dma((ITERS, 8)),
            dma((8,)),
            dma((8,)),
            dma(()),
            dma(()),
            dma(()),
            dma(()),
        ],
        compiler_params=pltpu.CompilerParams(collective_id=0, has_side_effects=True),
    )(coords, member, start_vector, self_block, neighbour_block, neighbours, coarse_map)


def solution(mesh):
    return jax.shard_map(
        functools.partial(local, mesh.shape["wide"], mesh.shape["narrow"]),
        mesh=mesh,
        in_specs=(
            P(None, "narrow", "wide"),
            P("narrow", "wide"),
            P(None, "narrow", "wide"),
            P(None, None, "narrow", "wide"),
            P(None, None, None, "narrow", "wide"),
            P(None, "narrow", "wide"),
            P(),
        ),
        out_specs=(
            P(None, None, None, "narrow", "wide"),
            P(None, "narrow", "wide"),
            P(None, ("wide", "narrow")),
        ),
        check_vma=False,
    )
```

time: 212 us -> 29.8 us (0.14)
  blocking collectives: 113 us -> 0 us
  starting transfers between devices: 40.7 us -> 0 us
  other arithmetic: 29.1 us -> 0 us
  Pallas kernels: 0 us -> 25.1 us
  waiting for transfers between devices: 12.3 us -> 0 us
  between operations: 8.01 us -> 0.64 us
  local copies, waits for them, and re-layouts: 6.97 us -> 3.87 us
    all_gather x1 -> x0, blocking collectives: 68.5 us -> none  [local(): lax.all_gather(factor_up.reshape(36, tiles_y * tiles_x), ('wide', 'narrow...]
    psum x1 -> x0, blocking collectives: 44.7 us -> none  [local(): lax.psum((jnp.stack(curvatures), jnp.stack(energies)), ('wide', 'narrow'))]
    ppermute x20 -> x0, starting transfers between devices: 40.7 us -> none  [the longest x10 27.8 us: extended_2(): before = lax.ppermute(last, axis, up)]
    pallas_call x0 -> x1, Pallas kernels: none -> 25.1 us  [local(): pl.pallas_call(functools.partial(kernel, wide, narrow, share), out_shape=...]
    another operation x10 -> x0, other arithmetic: 21.7 us -> none  [the longest x4 8.89 us: build_tentative(): factor_low = jnp.linalg.cholesky(gram_matrix)]
    ppermute x20 -> x0, waiting for transfers between devices: 12.3 us -> none  [the longest x10 9.88 us: extended_2(): after = lax.ppermute(initial, axis, down)]
  transfers between devices with their start and end apart: 20 -> 0, of which waited for: 6 -> 0; matrix products, arithmetic and copies ran while one was open for 16% -> 0% of each run, Pallas kernels for 0% -> 0%
where the time goes in v1:
time: 29.8 us; the launch traced here: 29.6 us
  Pallas kernels  25.1 us (84%)
  local copies, waits for them, and re-layouts  3.87 us (13%)
  between operations  0.64 us (2%)
    pallas_call x1, Pallas kernels, local(): pl.pallas_call(functools.partial(kernel, wide, narrow, share), out_shape=...  25.1 us
    unnamed x4, local copies, waits for them, and re-layouts  2.47 us
    pallas_call x1, local copies, waits for them, and re-layouts, local(): pl.pallas_call(functools.partial(kernel, wide, narrow, share), out_shape=...  1.4 us

profile of v1, /device:TPU:0, one launch (start us, length us, event | category | flops | bytes accessed | tf_op | source)
XLA Modules:
  0.0 29.6 jit_solution(1537467228362428063)
XLA Ops:
  0.6 25.1 %shard_map.94 = (f32[7,6,3,8,128]{4,3,2,1,0:T(8,128)}, f32[3,8,128]{2,1,0:T(8,128)}, f32[36,16]{1,0:T(8,128)}) custom-call(f32[3,8,128]{2,1,0:T(8,128)} %coords_h.1, s32[8,128]{1,0:T(8,128)} %member_h.1, f32[3,8,128]{2,1,0:T(8,128)} %start_h.1, f32[3,3,8,128]{3,2,1,0:T(8,128)} %self_h.1, f32[6,3,3,8,128]{4,3,2,1,0:T(8,128)} %nb_h.1, s32[6,8,128]{2,1,0:T(8,128)} %nbr_h.1, ...), custom_call_target="tpu_custom_call" | custom-call | tf_op jit(solution)/shard_map/pallas_call | solution.py:380
  25.7 1.4 %copy.10 = f32[36,16]{0,1:T(8,128)} copy(f32[36,16]{1,0:T(8,128)} %get-tuple-element.5) | data formatting | bytes 4608 | tf_op jit(solution)/shard_map/pallas_call | solution.py:380
  27.1 0.0 copy-start
  27.1 1.9 %copy.13 = f32[7,6,3,8,128]{4,3,2,1,0:T(8,128)} copy(f32[7,6,3,8,128]{4,3,2,1,0:T(8,128)} %get-tuple-element.9) | data formatting | bytes 1032192
  29.0 0.0 copy-done
  29.0 0.6 %copy.14 = f32[3,8,128]{2,1,0:T(8,128)} copy(f32[3,8,128]{2,1,0:T(8,128)S(1)} %copy-done) | data formatting | bytes 24576
Async XLA Ops:
  27.1 1.9 %copy-start = (f32[3,8,128]{2,1,0:T(8,128)S(1)}, f32[3,8,128]{2,1,0:T(8,128)}, u32[]{:S(2)}) copy-start(f32[3,8,128]{2,1,0:T(8,128)} %get-tuple-element.10) | copy-start | bytes 36868

commit v2 on v1

--- a/solution.py
+++ b/solution.py
@@ -13,6 +13,7 @@
 F32 = jnp.float32
 SUMS = 10
 FIELDS = 9
+START, SELF, NB = 0, 3, 12
 STEPS = [(-1, -1), (-1, 0), (-1, 1), (0, -1), (0, 1), (1, -1), (1, 0), (1, 1)]
 
 
@@ -42,9 +43,9 @@
     wide, narrow, share,
     coords_h, member_h, start_h, self_h, nb_h, nbr_h, cmap_h,
     out_ref, probe_ref, coarse_ref,
-    coords, member, selfb, nb, nbr, cmap,
-    its, edges, stencil, fields, pack, tedges, disp, mine, gath, sumrow, allsum, partial,
-    hrecv, vrecv, htrecv, vtrecv,
+    coords, member, nbr, cmap,
+    ext, wpack, stencil, fields, pack, tedges, disp, mine, gath, sumrow, allsum, partial,
+    wrecv, htrecv, vtrecv,
     in_sem, send_sem, recv_sem, tsend_sem, trecv_sem, gsend_sem, grecv_sem, ssend_sem, srecv_sem,
 ):
     count = wide * narrow
@@ -60,12 +61,20 @@
     def _(d):
         pl.semaphore_signal(barrier, inc=1, device_id=peer(d), device_id_type=MESH)
 
+    height, width = shape = member.shape
+    edge_count = nbr.shape[0]
+    codes_at = NB + 9 * edge_count
+    planes = codes_at + edge_count
+
+    def own(first, size):
+        return ext.at[first : first + size, 0:height, 0:width]
+
     loads = [
         pltpu.make_async_copy(src, dst, in_sem.at[i])
         for i, (src, dst) in enumerate(
             (
-                (coords_h, coords), (member_h, member), (start_h, its.at[0]), (nbr_h, nbr),
-                (self_h, selfb), (nb_h, nb), (cmap_h, cmap),
+                (nbr_h, nbr), (start_h, own(START, 3)), (self_h, own(SELF, 9)), (nb_h, own(NB, nb_h.shape[0])),
+                (coords_h, coords), (member_h, member), (cmap_h, cmap),
             )
         )
     ]
@@ -90,27 +99,52 @@
     for code in range(8):
         @pl.when(jnp.logical_not(present_at[code]))
         def _(code=code):
+            if code in (1, 6):
+                at = height + ITERS if code == 1 else height
+                ext[:, at : at + ITERS, 0:width] = jnp.zeros((planes, ITERS, width), F32)
+            else:
+                wrecv[code] = jnp.zeros(wrecv.shape[1:], F32)
             if code in (3, 4):
-                hrecv[:, code - 3] = jnp.zeros(hrecv.shape[:1] + hrecv.shape[2:], F32)
                 htrecv[code - 3] = jnp.zeros(htrecv.shape[1:], F32)
             else:
-                vrecv[:, code] = jnp.zeros(vrecv.shape[:1] + vrecv.shape[2:], F32)
                 vtrecv[code] = jnp.zeros(vtrecv.shape[1:], F32)
 
-    shape = member.shape
-    height, width = shape
     lane = lax.broadcasted_iota(jnp.int32, shape, 1)
     row = lax.broadcasted_iota(jnp.int32, shape, 0)
 
-    def edge_rows(values, number):
-        for r in range(3):
-            edges[number, r : r + 1, :] = values[r][:1]
-            edges[number, r + 4 : r + 5, :] = values[r][height - 1 :]
-
     for load in loads[:4]:
         load.wait()
-    start = [its[0, r] for r in range(3)]
-    edge_rows(start, 0)
+    for k in range(edge_count):
+        ext[codes_at + k, 0:height, 0:width] = nbr[k].astype(F32)
+    per = width // ITERS
+    for side in range(2):
+        for t in range(wpack.shape[1]):
+            tile = jnp.zeros(shape, F32)
+            for j, p in enumerate(range(t * per, min((t + 1) * per, planes))):
+                moved = roll(ext[p, 0:height, 0:width], ITERS * (j + side), 1)
+                tile = jnp.where(lane // ITERS == j, moved, tile)
+            wpack[side, t] = tile
+
+    pl.semaphore_wait(barrier, count - 1)
+
+    copies = []
+    for code in range(8):
+        dx = STEPS[code][1]
+        if dx == 0:
+            here, there = (0, height) if code == 1 else (height - ITERS, height + ITERS)
+            src = ext.at[:, here : here + ITERS, 0:width]
+            dst = ext.at[:, there : there + ITERS, 0:width]
+        else:
+            src, dst = wpack.at[0 if dx < 0 else 1], wrecv.at[7 - code]
+        copy = pltpu.make_async_remote_copy(
+            src_ref=src, dst_ref=dst, send_sem=send_sem.at[code], recv_sem=recv_sem.at[7 - code],
+            device_id=target(code), device_id_type=MESH,
+        )
+        pl.when(present_at[code])(copy.start)
+        copies.append(copy)
+
+    for load in loads[4:]:
+        load.wait()
     present = member[...].astype(F32)
     x, y, z = (coords[r] * present for r in range(3))
     products = [present * present, x * present, y * present, z * present, x * x, y * y, z * z, x * y, x * z, y * z]
@@ -166,33 +200,12 @@
     mine[1:2] = rows_out[1]
     gath[me] = jnp.concatenate(rows_out, axis=0)
 
-    pl.semaphore_wait(barrier, count - 1)
-
-    def send_halo(number):
-        copies = []
-        for code in range(8):
-            if code in (3, 4):
-                src, dst = its.at[number], hrecv.at[number, 4 - code]
-            else:
-                src, dst = edges.at[number], vrecv.at[number, 7 - code]
-            copy = pltpu.make_async_remote_copy(
-                src_ref=src, dst_ref=dst, send_sem=send_sem.at[number, code], recv_sem=recv_sem.at[number, 7 - code],
-                device_id=target(code), device_id_type=MESH,
-            )
-            pl.when(present_at[code])(copy.start)
-            copies.append(copy)
-        return copies
-
-    def wait_halo(number, recv, hbuf, vbuf):
-        for code in range(8):
-            if code in (3, 4):
-                ref = hbuf.at[code - 3]
-            else:
-                ref = vbuf.at[code]
-            arrival = pltpu.make_async_copy(ref, ref, recv(code))
+    def wait_halo(codes, recv, ref_of):
+        for code in codes:
+            ref = ref_of(code)
+            arrival = pltpu.make_async_copy(ref, ref, recv.at[code])
             pl.when(present_at[code])(arrival.wait)
 
-    sent = [send_halo(0)]
     tcopies = []
     for code in range(8):
         if code in (3, 4):
@@ -213,46 +226,86 @@
             device_id=peer(d), device_id_type=MESH,
         ).start()
 
-    for load in loads[4:]:
-        load.wait()
-    edge_count = nb.shape[0]
-    for code in range(8):
-        masks = [nbr[k] == code for k in range(edge_count)]
-        for r in range(3):
-            for s in range(3):
+    def by_displacement(r0, c0):
+        def at(p):
+            return ext[p, r0 : r0 + height, c0 : c0 + width]
+
+        for code in range(8):
+            masks = [at(codes_at + k) == code for k in range(edge_count)]
+            for q in range(9):
                 value = jnp.zeros(shape, F32)
                 for k in range(edge_count):
-                    value = jnp.where(masks[k], nb[k, r, s], value)
-                stencil[code, 3 * r + s] = value
-    diag = [selfb[r, r] for r in range(3)]
-    inv = [1.0 / d for d in diag]
-
-    iterate = start
+                    value = jnp.where(masks[k], at(NB + 9 * k + q), value)
+                stencil[code, q, r0 : r0 + height, c0 : c0 + width] = value
+
+    def ring(code):
+        at = height + ITERS if code == 1 else height
+        return ext.at[:, at : at + ITERS, 0:width]
+
+    by_displacement(0, 0)
+    wait_halo((1, 6), recv_sem, ring)
+    by_displacement(height, 0)
+    wait_halo((0, 2, 3, 4, 5, 7), recv_sem, lambda code: wrecv.at[code])
+    half = row < ITERS
+    for t in range(wpack.shape[1]):
+        pairs = (
+            (wrecv[4, t], wrecv[3, t]),
+            (jnp.where(half, wrecv[7, t], wrecv[2, t]), jnp.where(half, wrecv[5, t], wrecv[0, t])),
+        )
+        for j, p in enumerate(range(t * per, min((t + 1) * per, planes))):
+            for r0, (right, left) in zip((0, height), pairs):
+                tile = jnp.where(lane >= width - ITERS, roll(left, -ITERS * (j + 1), 1), 0.0)
+                ext[p, r0 : r0 + height, width:] = jnp.where(lane < ITERS, roll(right, -ITERS * j, 1), tile)
+    by_displacement(0, width)
+    by_displacement(height, width)
+
+    def full(p):
+        return ext[p]
+
+    selfb = {(r, s): (lambda r=r, s=s: ext[SELF + 3 * r + s, 0:height, 0:width]) for r in range(3) for s in range(3)}
+    nb = {
+        (k, r, s): (lambda k=k, r=r, s=s: ext[NB + 9 * k + 3 * r + s, 0:height, 0:width])
+        for k in range(edge_count) for r in range(3) for s in range(3)
+    }
+    elane = lax.broadcasted_iota(jnp.int32, (2 * height, 2 * width), 1)
+    erow = lax.broadcasted_iota(jnp.int32, (2 * height, 2 * width), 0)
+
+    def between(value, low, high):
+        return jnp.logical_and(value >= low, value < high)
+
+    last_row = jnp.where(me_n < narrow - 1, height + ITERS, height)
+    back_row = jnp.where(me_n > 0, height + ITERS, 2 * height)
+    last_lane = jnp.where(me_w < wide - 1, width + ITERS, width)
+    back_lane = jnp.where(me_w > 0, 2 * width - ITERS, 2 * width)
+    inside = jnp.logical_and(
+        jnp.logical_or(erow < last_row, erow >= back_row), jnp.logical_or(elane < last_lane, elane >= back_lane)
+    )
+    inverse = [jnp.where(inside, 1.0 / full(SELF + 4 * r), 0.0) for r in range(3)]
+    diag = [selfb[r, r]() for r in range(3)]
+    inv = [inverse[r][:height, :width] for r in range(3)]
+
+    iterate = [full(START + r) for r in range(3)]
     for number in range(ITERS):
-        wait_halo(number, lambda code: recv_sem.at[number, code], hrecv.at[number], vrecv.at[number])
-        applied = [sum(selfb[r, s] * iterate[s] for s in range(3)) for r in range(3)]
+        final = number == ITERS - 1
+        rs, cs = (slice(0, height), slice(0, width)) if final else (slice(None), slice(None))
+        applied = [sum(ext[SELF + 3 * r + s, rs, cs] * iterate[s][rs, cs] for s in range(3)) for r in range(3)]
         for s in range(3):
-            rows = {
-                code: vrecv[number, code, (s + 4 if code < 3 else s) : (s + 5 if code < 3 else s + 1), :]
-                for code in (0, 1, 2, 5, 6, 7)
-            }
-            moved = displaced(
-                iterate[s], roll(hrecv[number, 0, s], 1, 1), roll(hrecv[number, 1, s], -1, 1), rows, lane, row
-            )
-            for r in range(3):
-                for code in range(8):
-                    applied[r] = applied[r] + stencil[code, 3 * r + s] * moved[code]
-        following = [applied[r] * inv[r] for r in range(3)]
-        if number < ITERS - 1:
-            for r in range(3):
-                its[number + 1, r] = following[r]
-            edge_rows(following, number + 1)
-            sent.append(send_halo(number + 1))
-        curvature = sum(iterate[r] * applied[r] for r in range(3))
-        energy = sum(iterate[r] * diag[r] * iterate[r] for r in range(3))
+            for dy in (-1, 0, 1):
+                shifted = roll(iterate[s], -dy, 0)
+                for dx in (-1, 0, 1):
+                    if (dy, dx) == (0, 0):
+                        continue
+                    code = STEPS.index((dy, dx))
+                    moved = roll(shifted, -dx, 1)[rs, cs]
+                    for r in range(3):
+                        applied[r] = applied[r] + stencil[code, 3 * r + s, rs, cs] * moved
+        mine_it = [v[:height, :width] for v in iterate]
+        mine_ap = [v[:height, :width] for v in applied]
+        curvature = sum(mine_it[r] * mine_ap[r] for r in range(3))
+        energy = sum(mine_it[r] * diag[r] * mine_it[r] for r in range(3))
         partial[number : number + 1] = jnp.sum(curvature, axis=0, keepdims=True)
         partial[number + 4 : number + 5] = jnp.sum(energy, axis=0, keepdims=True)
-        iterate = following
+        iterate = [applied[r] * (inv[r] if final else inverse[r]) for r in range(3)]
 
     totals = jnp.sum(partial[...], axis=1, keepdims=True)
     line = jnp.sum(jnp.where(lane == row, totals, 0.0), axis=0, keepdims=True)
@@ -266,7 +319,7 @@
             device_id=peer(d), device_id_type=MESH,
         ).start()
 
-    wait_halo(0, lambda code: trecv_sem.at[code], htrecv, vtrecv)
+    wait_halo(range(8), trecv_sem, lambda code: htrecv.at[code - 3] if code in (3, 4) else vtrecv.at[code])
     lpack, rpack = htrecv[0], htrecv[1]
     for j in range(FIELDS):
         rows = {code: vtrecv[code, j : j + 1, :] for code in (0, 1, 2, 5, 6, 7)}
@@ -285,7 +338,7 @@
             out_ref[index, 4, r] = c0 * b0 + c1 * b1 + c2 * b2
             out_ref[index, 5, r] = c0 * g0 + c1 * g1 + c2 * g2
 
-    piece(lambda r, s: selfb[r, s], [fields[j] for j in range(FIELDS)], 0)
+    piece(lambda r, s: selfb[r, s](), [fields[j] for j in range(FIELDS)], 0)
     for k in range(edge_count):
         masks = [nbr[k] == code for code in range(1, 8)]
         picked = []
@@ -294,7 +347,7 @@
             for code in range(1, 8):
                 value = jnp.where(masks[code - 1], disp[j, code], value)
             picked.append(value)
-        piece(lambda r, s: nb[k, r, s], picked, k + 1)
+        piece(lambda r, s: nb[k, r, s](), picked, k + 1)
 
     some = gath.at[pl.ds(0, count - 1)]
     pltpu.make_async_copy(some, some, grecv_sem).wait()
@@ -311,23 +364,24 @@
         take = jnp.logical_and(crow == j, cgroup == lax.rem(tile_col, tiles_x))
         low = jnp.where(take, lines[0:1], low)
         high = jnp.where(take, lines[1:2], high)
-    pick = (lax.broadcasted_iota(jnp.int32, (8, width), 1) % 8 == lax.broadcasted_iota(jnp.int32, (8, width), 0)).astype(F32)
-    low, high = (
-        lax.dot_general(
-            pick, v, (((1,), (1,)), ((), ())), precision=lax.Precision.HIGHEST, preferred_element_type=F32
-        )
-        for v in (low, high)
-    )
-    l00, mx, my, mz, l33, l43, l53, l44 = (low[q : q + 1] for q in range(8))
-    l54, l55 = high[0:1], high[1:2]
-    coarse_ref[...] = jnp.zeros(coarse_ref.shape, F32)
+    l00, mx, my, mz, l33, l43, l53, l44, l54, l55 = range(SUMS)
     entries = {
-        (0, 0): l00, (1, 1): l00, (2, 2): l00,
-        (3, 0): -my, (3, 1): mx, (4, 1): -mz, (4, 2): my, (5, 0): mz, (5, 2): -mx,
-        (3, 3): l33, (4, 3): l43, (5, 3): l53, (4, 4): l44, (5, 4): l54, (5, 5): l55,
+        (0, 0): (l00, 1), (1, 1): (l00, 1), (2, 2): (l00, 1),
+        (3, 0): (my, -1), (3, 1): (mx, 1), (4, 1): (mz, -1), (4, 2): (my, 1), (5, 0): (mz, 1), (5, 2): (mx, -1),
+        (3, 3): (l33, 1), (4, 3): (l43, 1), (5, 3): (l53, 1), (4, 4): (l44, 1), (5, 4): (l54, 1), (5, 5): (l55, 1),
     }
-    for (n, m), entry in entries.items():
-        coarse_ref[6 * m + n : 6 * m + n + 1, :] = entry
+    outs = coarse_ref.shape[1]
+    kind = lax.broadcasted_iota(jnp.int32, (1, outs), 1)
+    chosen, sign = jnp.full((1, outs), -1, jnp.int32), jnp.zeros((1, outs), F32)
+    for (n, m), (q, way) in entries.items():
+        chosen = jnp.where(kind == 6 * m + n, q, chosen)
+        sign = jnp.where(kind == 6 * m + n, float(way), sign)
+    entry = lax.broadcasted_iota(jnp.int32, (width, outs), 0) % 8
+    coarse = jnp.zeros(coarse_ref.shape, F32)
+    for base, lines in ((0, low), (8, high)):
+        pick = jnp.where(entry + base == chosen, sign, 0.0)
+        coarse = coarse + jnp.dot(lines, pick, precision=lax.Precision.HIGHEST, preferred_element_type=F32)
+    coarse_ref[...] = coarse
 
     some = allsum.at[pl.ds(0, count - 1)]
     pltpu.make_async_copy(some, some, srecv_sem).wait()
@@ -361,9 +415,9 @@
             for r in range(3):
                 out_ref[k, m, r] = out_ref[k, m, r] * weight
 
-    for copies in sent + [tcopies]:
+    for some in (copies, tcopies):
         for code in range(8):
-            pl.when(present_at[code])(copies[code].wait_send)
+            pl.when(present_at[code])(some[code].wait_send)
     for buffer, sem in ((gath, gsend_sem), (allsum, ssend_sem)):
         some = buffer.at[pl.ds(0, count - 1)]
         pltpu.make_async_copy(some, some, sem).wait()
@@ -375,27 +429,28 @@
     count = wide * narrow
     share = coarse_map.shape[0] // count
     tile = (height, width)
+    double = (2 * height, 2 * width)
+    planes = 12 + 10 * edge_count
+    packs = pl.cdiv(planes, width // ITERS)
     vmem = pltpu.VMEM
     dma = pltpu.SemaphoreType.DMA
-    return pl.pallas_call(
+    smoothed, probe, coarse = pl.pallas_call(
         functools.partial(kernel, wide, narrow, share),
         out_shape=(
             jax.ShapeDtypeStruct((edge_count + 1, 6, 3) + tile, F32),
             jax.ShapeDtypeStruct((3,) + tile, F32),
-            jax.ShapeDtypeStruct((36, share), F32),
+            jax.ShapeDtypeStruct((share, 36), F32),
         ),
         in_specs=[pl.BlockSpec(memory_space=pl.ANY)] * 7,
         out_specs=(pl.BlockSpec(memory_space=pltpu.VMEM),) * 3,
         scratch_shapes=[
             vmem((3,) + tile, F32),
             vmem(tile, jnp.int32),
-            vmem((3, 3) + tile, F32),
-            vmem((edge_count, 3, 3) + tile, F32),
             vmem((edge_count,) + tile, jnp.int32),
             pltpu.SMEM(coarse_map.shape, jnp.int32),
-            vmem((ITERS, 3) + tile, F32),
-            vmem((ITERS, 8, width), F32),
-            vmem((8, 9) + tile, F32),
+            vmem((planes,) + double, F32),
+            vmem((2, packs) + tile, F32),
+            vmem((8, 9) + double, F32),
             vmem((FIELDS,) + tile, F32),
             vmem((2,) + tile, F32),
             vmem((2, 16, width), F32),
@@ -405,13 +460,12 @@
             vmem((1, width), F32),
             vmem((count, 1, width), F32),
             vmem((8, width), F32),
-            vmem((ITERS, 2, 3) + tile, F32),
-            vmem((ITERS, 8, 8, width), F32),
+            vmem((8, packs) + tile, F32),
             vmem((2,) + tile, F32),
             vmem((8, 16, width), F32),
             dma((7,)),
-            dma((ITERS, 8)),
-            dma((ITERS, 8)),
+            dma((8,)),
+            dma((8,)),
             dma((8,)),
             dma((8,)),
             dma(()),
@@ -420,7 +474,11 @@
             dma(()),
         ],
         compiler_params=pltpu.CompilerParams(collective_id=0, has_side_effects=True),
-    )(coords, member, start_vector, self_block, neighbour_block, neighbours, coarse_map)
+    )(
+        coords, member, start_vector, self_block.reshape((9,) + tile), neighbour_block.reshape((-1,) + tile),
+        neighbours, coarse_map,
+    )
+    return smoothed, probe, coarse.T
 
 
 def solution(mesh):

time: 29.8 us -> 23.3 us (0.78)
  Pallas kernels: 25.1 us -> 19.2 us
  local copies, waits for them, and re-layouts: 3.87 us -> 3.17 us
    pallas_call x1, Pallas kernels: 25.1 us -> 19.2 us  [local(): pl.pallas_call(functools.partial(kernel, wide, narrow, share), out_shape=...]
    pallas_call x1 -> x0, local copies, waits for them, and re-layouts: 1.4 us -> none  [local(): pl.pallas_call(functools.partial(kernel, wide, narrow, share), out_shape=...]
    unnamed x4 -> x7, local copies, waits for them, and re-layouts: 2.47 us -> 3.17 us
where the time goes in v2:
time: 23.3 us; the launch traced here: 23.1 us
  Pallas kernels  19.2 us (82%)
  local copies, waits for them, and re-layouts  3.17 us (14%)
  between operations  0.65 us (3%)
    pallas_call x1, Pallas kernels, local(): pl.pallas_call(functools.partial(kernel, wide, narrow, share), out_shape=...  19.2 us
    unnamed x7, local copies, waits for them, and re-layouts  3.17 us

profile of v2, /device:TPU:0, one launch (start us, length us, event | category | flops | bytes accessed | tf_op | source)
XLA Modules:
  0.0 23.1 jit_solution(10857659955847860108)
XLA Ops:
  0.6 19.2 %shard_map.94 = (f32[7,6,3,8,128]{4,3,2,1,0:T(8,128)}, f32[3,8,128]{2,1,0:T(8,128)}, f32[16,36]{1,0:T(8,128)}) custom-call(f32[3,8,128]{2,1,0:T(8,128)} %coords_h.1, s32[8,128]{1,0:T(8,128)} %member_h.1, f32[3,8,128]{2,1,0:T(8,128)} %start_h.1, f32[9,8,128]{2,1,0:T(8,128)} %bitcast.4, f32[54,8,128]{2,1,0:T(8,128)} %bitcast.3, s32[6,8,128]{2,1,0:T(8,128)} %nbr_h.1, ...), custom_call_target="tpu_custom_call" | custom-call | tf_op jit(solution)/shard_map/pallas_call | solution.py:437
  19.9 0.0 copy-start
  19.9 1.9 %copy.13 = f32[7,6,3,8,128]{4,3,2,1,0:T(8,128)} copy(f32[7,6,3,8,128]{4,3,2,1,0:T(8,128)} %get-tuple-element.12) | data formatting | bytes 1032192
  21.7 0.0 copy-done
  21.7 0.0 copy-start.1
  21.8 0.6 %copy.14 = f32[3,8,128]{2,1,0:T(8,128)} copy(f32[3,8,128]{2,1,0:T(8,128)S(1)} %copy-done) | data formatting | bytes 24576
  22.4 0.1 copy-done.1
  22.5 0.6 %copy.15 = f32[36,16]{0,1:T(8,128)} copy(f32[36,16]{0,1:T(8,128)S(1)} %bitcast.5) | data formatting | bytes 4608
Async XLA Ops:
  19.9 1.9 %copy-start = (f32[3,8,128]{2,1,0:T(8,128)S(1)}, f32[3,8,128]{2,1,0:T(8,128)}, u32[]{:S(2)}) copy-start(f32[3,8,128]{2,1,0:T(8,128)} %get-tuple-element.13) | copy-start | bytes 36868
  21.7 0.7 %copy-start.1 = (f32[16,36]{1,0:T(8,128)S(1)}, f32[16,36]{1,0:T(8,128)}, u32[]{:S(2)}) copy-start(f32[16,36]{1,0:T(8,128)} %get-tuple-element.8) | copy-start | bytes 6916
